TPU v7x, 512 devices: a 4x2x32 block of a 4x16x32 slice. The times are simulated.
512 devices in a mesh: groups: 2 (over y), expert: 64 (over z, core), hidden: 4 (over x).
Axes of the slice: x: 4, y: 2, z: 32, core: 2. Of those that a mesh axis runs over, the one named last changes fastest.
The devices are a block of a 4x16x32 slice.
Arguments:
- tokens: bfloat16 [2048, 4096], P(('groups', 'expert')), parts along dimension 0, may hold values from -6 to 6
- expert_ids: int32 [2048, 8], P(('groups', 'expert')), parts along dimension 0, may hold values from 0 to 31, all different within a row; in each aligned block of 16 rows (0 to 15, 16 to 31, ...) at most 8 rows name the same one
- router_scores: float32 [2048, 8], P(('groups', 'expert')), parts along dimension 0, may hold values from 0.05 to 1
- gate_weight: bfloat16 [64, 4096, 512], P('expert', None, 'hidden'), may hold values from -0.09375 to 0.09375
- up_weight: bfloat16 [64, 4096, 512], P('expert', None, 'hidden'), may hold values from -0.09375 to 0.09375
- down_weight: bfloat16 [64, 512, 4096], P('expert', 'hidden'), may hold values from -0.1875 to 0.1875
Outputs:
- moe_out: bfloat16 [2048, 4096], P(('groups', 'expert'), 'hidden'), parts along dimension 0
There are 2 independent parts, one for each index of `groups`. A program takes and returns all parts, laid end to end along the dimension named above; an argument that names none is the same for every part. Nothing has to cross between parts.
Inputs may be any that keep to these rules, and one draw needn't show every extreme that they name: `expert_ids`: each row names 8 different experts. In each aligned block of 16 rows no expert is named by more than 8 rows, a bound that some block reaches.
All inputs are finite; a program needn't handle non-finite values.
Results may differ from a plain program's by a relative error of at most 0.012.
Values may be sent and summed in bfloat16 or wider, within the bound.
No kernel may reach another device: no remote copies, remote signals or barrier semaphores. Data moves between devices by JAX's collectives and lax.ppermute only.
A program may use at most 64 MiB of HBM per device.

v0:
```python
import jax
import jax.numpy as jnp
from jax import lax
from jax.sharding import PartitionSpec as P

SPAN = 2


def split_up(x, dim, length):
    shape = x.shape
    blocks = x.reshape(*shape[:dim], length, shape[dim] // length, *shape[dim + 1 :])
    return jnp.moveaxis(blocks, dim, 0)


def sent_and_summed(x, axis, dim):
    blocks = split_up(x, dim, lax.axis_size(axis))
    arrived = lax.all_to_all(blocks, axis, split_axis=0, concat_axis=0, tiled=True)
    return arrived.astype(jnp.float32).sum(axis=0)


def capacity(tok_count, top_count, expert_count):
    return max(2, min(tok_count, 2 * tok_count * top_count // expert_count))


def slot_numbers(expert_ids, expert_count, slot_cap):
    pair_ids = expert_ids.reshape(-1)
    onehot = (pair_ids[:, None] == jnp.arange(expert_count, dtype=jnp.int32)[None, :]).astype(
        jnp.int32
    )
    before = jnp.cumsum(onehot, axis=0) - onehot
    return pair_ids * slot_cap + jnp.sum(before * onehot, axis=1)


def expert_rows(received, gate_weight, up_weight, down_weight):
    source_count, row_count, model_width = received.shape
    row_block = received.reshape(source_count * row_count, model_width)
    gate_val = jnp.dot(row_block, gate_weight[0], preferred_element_type=jnp.float32)
    up_val = jnp.dot(row_block, up_weight[0], preferred_element_type=jnp.float32)
    activated = (jax.nn.silu(gate_val) * up_val).astype(jnp.bfloat16)
    pieces = jnp.dot(activated, down_weight[0], preferred_element_type=jnp.float32).astype(
        jnp.bfloat16
    )
    return pieces.reshape(source_count, row_count, model_width)


def body(tokens, expert_ids, router_scores, gate_weight, up_weight, down_weight):
    tok_count, model_width = tokens.shape
    top_count = expert_ids.shape[1]
    slots_all = lax.axis_size("expert")
    experts = slots_all // SPAN
    slot_cap = capacity(tok_count, top_count, experts)
    slot_index = slot_numbers(expert_ids, experts, slot_cap)
    token_of_pair = jnp.arange(tok_count * top_count, dtype=jnp.int32) // top_count
    owner_row = (
        jnp.full((experts * slot_cap,), tok_count, jnp.int32).at[slot_index].set(token_of_pair)
    )
    padded = jnp.concatenate([tokens, jnp.zeros((1, model_width), tokens.dtype)], axis=0)
    packed = padded[owner_row].reshape(experts, slot_cap, model_width)
    column_width = model_width // lax.axis_size("hidden")
    column_start = lax.axis_index("hidden") * column_width
    narrow = lax.dynamic_slice_in_dim(packed, column_start, column_width, 2)
    outgoing = jnp.repeat(narrow, SPAN, axis=0)
    widened = lax.all_gather(
        lax.all_to_all(outgoing, "expert", split_axis=0, concat_axis=0, tiled=True),
        "hidden",
        axis=2,
        tiled=True,
    )
    pieces = expert_rows(widened, gate_weight, up_weight, down_weight)
    routed = 2.5 * router_scores / jnp.sum(router_scores, axis=1, keepdims=True)
    reduced = sent_and_summed(pieces.astype(jnp.float32).astype(jnp.bfloat16), "hidden", 2)
    returned = lax.all_to_all(
        reduced.astype(jnp.bfloat16), "expert", split_axis=0, concat_axis=0, tiled=True
    ).astype(reduced.dtype)
    columns = returned.shape[2]
    summed = jnp.sum(returned.reshape(experts, SPAN, slot_cap, columns), axis=1).reshape(
        experts * slot_cap, columns
    )
    picked = summed[slot_index].reshape(tok_count, top_count, columns)
    result = jnp.sum(routed[:, :, None] * picked, axis=1)
    return result.astype(jnp.bfloat16)


def solution(mesh):
    return jax.shard_map(
        body,
        mesh=mesh,
        in_specs=(
            P(("groups", "expert"), None),
            P(("groups", "expert"), None),
            P(("groups", "expert"), None),
            P("expert", None, "hidden"),
            P("expert", None, "hidden"),
            P("expert", "hidden", None),
        ),
        out_specs=P(("groups", "expert"), "hidden"),
        check_vma=False,
    )
```

profile of v0, /device:TPU:40, one launch (start us, length us, event | category | flops | bytes accessed | tf_op | source)
XLA Modules:
  0.0 429.7 jit_solution(12580211501950943718)
XLA Ops:
  6.5 0.0 copy-start
  6.6 0.0 all-gather.2.cloned.1.call-start
  6.6 0.8 copy.19
  7.4 0.7 broadcast_multiply_fusion
  8.1 0.1 eq.15
  8.2 0.1 fusion.23
  8.3 0.2 reduce_window_sum.11
  8.4 0.2 select_reduce_fusion
  8.6 0.1 copy.18
  8.7 0.1 mul.48
  8.8 1.0 scatter_custom_fusion
  9.8 0.9 concatenate.3
  10.7 1.8 gather_fusion
  12.6 0.0 copy-start.1
  12.7 0.1 broadcast_in_dim.8
  12.8 0.0 copy-start.2
  12.8 156.5 %all_to_all.15 = bf16[64,8,1024]{2,1,0:T(8,128)(2,1)} all-to-all(bf16[64,8,1024]{2,1,0:T(8,128)(2,1)S(1)} %bitcast.44), channel_id=1, replica_groups=mesh['groups'=2,'expert'=64,'hidden'=4] {'expert'}, dimensions={0} | all-to-all | bytes 2097152 | tf_op jit(solution)/shard_map/all_to_all | solution.py:64
  169.3 0.1 all-gather.2.cloned.1.call-update
  169.4 46.0 %all-gather.2.cloned.1.call-done = bf16[64,8,4096]{2,1,0:T(8,128)(2,1)} async-done(((bf16[64,8,1024]{2,1,0:T(8,128)(2,1)}), bf16[64,8,4096]{2,1,0:T(8,128)(2,1)}) %all-gather.2.cloned.1.call-update) | async-done | bytes 4194320 | tf_op jit(solution)/shard_map/all_gather | solution.py:63
  215.4 0.0 copy-done.1
  215.4 3.4 fusion.2
  218.8 0.0 copy-done
  218.8 0.0 copy-done.2
  218.8 8.6 %convolution_convert_fusion = bf16[512,4096]{1,0:T(8,128)(2,1)} fusion(bf16[64,8,4096]{2,1,0:T(8,128)(2,1)} %all-gather.2.cloned.1.call-done, bf16[1,128,4096]{2,1,0:T(8,128)(2,1)S(1)} %copy-done, bf16[1,4096,128]{2,1,0:T(8,128)(2,1)S(1)} %copy-done.2, f32[512,128]{1,0:T(8,128)S(1)} %fusion.2), kind=kOutput, calls=%fused_computation.3 | convolution fusion | flops 1076232192 | bytes 10747904 | tf_op jit(solution)/shard_map/dot_general | solution.py:40
  227.5 2.6 copy.22
  230.1 52.4 %all_to_all.16 = bf16[4,64,8,1024]{3,2,1,0:T(8,128)(2,1)} all-to-all(bf16[4,64,8,1024]{3,2,1,0:T(8,128)(2,1)S(1)} %bitcast.42), channel_id=1, replica_groups=mesh['groups'=2,'expert'=64,'hidden'=4] {'hidden'}, dimensions={0} | all-to-all | bytes 8388608 | tf_op jit(solution)/shard_map/all_to_all | solution.py:17
  282.5 0.0 copy-start.3
  282.5 4.4 %reduce_sum.53 = bf16[64,8,1024]{2,1,0:T(8,128)(2,1)} reduce(bf16[4,64,8,1024]{3,2,1,0:T(8,128)(2,1)} %all_to_all.16, bf16[]{:T(256)} %constant.21.clone.1), dimensions={0}, to_apply=%region_4.5 | reduce | flops 1572864 | bytes 5242882 | tf_op jit(solution)/shard_map/reduce_sum | solution.py:18
  286.9 24.9 %all-to-all-start.2 = ((bf16[64,8,1024]{2,1,0:T(8,128)(2,1)}), bf16[64,8,1024]{2,1,0:T(8,128)(2,1)S(1)}, u32[]{:S(2)}, u32[]{:S(2)}) async-start(bf16[64,8,1024]{2,1,0:T(8,128)(2,1)} %reduce_sum.53), calls=%async_computation.2 | async-start | bytes 2097152 | tf_op jit(solution)/shard_map/all_to_all | solution.py:72
  311.8 0.0 copy-done.3
  311.8 0.1 copy.17
  311.9 109.0 %all-to-all-done.2 = bf16[64,8,1024]{2,1,0:T(8,128)(2,1)S(1)} async-done(((bf16[64,8,1024]{2,1,0:T(8,128)(2,1)}), bf16[64,8,1024]{2,1,0:T(8,128)(2,1)S(1)}, u32[]{:S(2)}, u32[]{:S(2)}) %all-to-all-start.2) | async-done | bytes 1048608 | tf_op jit(solution)/shard_map/all_to_all | solution.py:72
  420.9 0.2 convert_reduce_fusion
  421.2 0.8 gather_fusion.1
  422.0 0.8 fusion.16
  (8 shorter events, 0.1 us)
Async XLA Ops:
  6.5 212.3 %copy-start = (bf16[1,128,4096]{2,1,0:T(8,128)(2,1)S(1)}, bf16[1,128,4096]{2,1,0:T(8,128)(2,1)}, u32[]{:S(2)}) copy-start(bf16[1,128,4096]{2,1,0:T(8,128)(2,1)} %param.11) | copy-start | bytes 3145732
  6.6 208.8 %all-gather.2.cloned.1.call-start = ((), (), s32[]{:S(2)}) async-start(), calls=%async_computation.3 | async-start | bytes 5242880 | tf_op jit(solution)/shard_map/all_gather | solution.py:63
  12.6 202.7 %copy-start.1 = (bf16[1,4096,128]{2,1,0:T(8,128)(2,1)S(1)}, bf16[1,4096,128]{2,1,0:T(8,128)(2,1)}, u32[]{:S(2)}) copy-start(bf16[1,4096,128]{2,1,0:T(8,128)(2,1)} %param.9) | copy-start | bytes 3145732
  12.8 206.0 %copy-start.2 = (bf16[1,4096,128]{2,1,0:T(8,128)(2,1)S(1)}, bf16[1,4096,128]{2,1,0:T(8,128)(2,1)}, u32[]{:S(2)}) copy-start(bf16[1,4096,128]{2,1,0:T(8,128)(2,1)} %param.10) | copy-start | bytes 3145732
  282.5 29.3 %copy-start.3 = (f32[16,8]{0,1:T(8,128)S(1)}, f32[16,8]{0,1:T(8,128)}, u32[]{:S(2)}) copy-start(f32[16,8]{0,1:T(8,128)} %param.8) | copy-start | bytes 1540
  286.9 134.0 %all-to-all-start.2 = ((bf16[64,8,1024]{2,1,0:T(8,128)(2,1)}), bf16[64,8,1024]{2,1,0:T(8,128)(2,1)S(1)}, u32[]{:S(2)}, u32[]{:S(2)}) async-start(bf16[64,8,1024]{2,1,0:T(8,128)(2,1)} %reduce_sum.53), calls=%async_computation.2 | async-start | bytes 2097152 | tf_op jit(solution)/shard_map/all_to_all | solution.py:72
Sparse Core Ops, SparseCore 0:
  169.5 45.8 all-gather.1
where the time goes:
time: 430 us
  blocking collectives  209 us (49%)
  waiting for transfers between devices  155 us (36%)
  starting transfers between devices  24.9 us (6%)
  between operations  13.6 us (3%)
  matrix products  12.1 us (3%)
  local copies, waits for them, and re-layouts  8.53 us (2%)
  other arithmetic  6.62 us (2%)
    all_to_all x1, blocking collectives, body(): lax.all_to_all(outgoing, 'expert', split_axis=0, concat_axis=0, tiled=True)  157 us
    all_to_all x1, waiting for transfers between devices, body(): lax.all_to_all(reduced.astype(jnp.bfloat16), 'expert', split_axis=0, conc...  109 us
    all_to_all x1, blocking collectives, sent_and_summed(): lax.all_to_all(blocks, axis, split_axis=0, concat_axis=0, tiled=True)  52.4 us
    all_gather x1, waiting for transfers between devices, body(): lax.all_gather(lax.all_to_all(outgoing, 'expert', split_axis=0, concat_ax...  46 us
    all_to_all x1, starting transfers between devices, body(): lax.all_to_all(reduced.astype(jnp.bfloat16), 'expert', split_axis=0, conc...  24.9 us
    dot_general x1, matrix products, expert_rows(): jnp.dot(activated, down_weight[0], preferred_element_type=jnp.float32)  8.64 us
  transfers between devices with their start and end apart: 2, of which 2 were waited for; matrix products, arithmetic and copies ran while one was open for 0% of the time, Pallas kernels for 0%

commit v1 on v0

v1 whole, which is shorter than its diff:
```python
import jax
import jax.numpy as jnp
from jax import lax
from jax.sharding import PartitionSpec as P

SPAN = 2


def body(tokens, expert_ids, router_scores, gate_weight, up_weight, down_weight):
    experts = lax.axis_size("expert") // SPAN
    rows = lax.all_gather(tokens, "expert", axis=0, tiled=True)
    routed = 2.5 * router_scores / jnp.sum(router_scores, axis=1, keepdims=True)
    named = expert_ids[:, :, None] == jnp.arange(experts, dtype=jnp.int32)[None, None, :]
    weight_table = jnp.sum(jnp.where(named, routed[:, :, None], 0.0), axis=1)
    weights_all = lax.all_gather(weight_table, "expert", axis=0, tiled=True)
    mine = lax.axis_index("expert") // SPAN
    weight_col = lax.dynamic_slice_in_dim(weights_all, mine, 1, 1)
    down = lax.all_to_all(down_weight[0], "hidden", split_axis=1, concat_axis=0, tiled=True)
    both = jnp.concatenate([gate_weight[0], up_weight[0]], axis=1)
    width = gate_weight.shape[2]
    val = jnp.dot(rows, both, preferred_element_type=jnp.float32)
    act = (jax.nn.silu(val[:, :width]) * val[:, width:]).astype(jnp.bfloat16)
    act_all = lax.all_gather(act, "hidden", axis=1, tiled=True)
    out = jnp.dot(act_all, down, preferred_element_type=jnp.float32)
    out = (out * weight_col).astype(jnp.bfloat16)
    return lax.psum_scatter(out, "expert", scatter_dimension=0, tiled=True)


def solution(mesh):
    return jax.shard_map(
        body,
        mesh=mesh,
        in_specs=(
            P(("groups", "expert"), None),
            P(("groups", "expert"), None),
            P(("groups", "expert"), None),
            P("expert", None, "hidden"),
            P("expert", None, "hidden"),
            P("expert", "hidden", None),
        ),
        out_specs=P(("groups", "expert"), "hidden"),
        check_vma=False,
    )
```

time: 430 us -> 459 us (1.067)
  waiting for transfers between devices: 155 us -> 372 us
  blocking collectives: 209 us -> 55 us
  starting transfers between devices: 24.9 us -> 4.31 us
  local copies, waits for them, and re-layouts: 8.53 us -> 2.37 us
  other arithmetic: 6.62 us -> 1 us
    all_to_all x2 -> x0, blocking collectives: 209 us -> none  [the longest x1 157 us: body(): lax.all_to_all(outgoing, 'expert', split_axis=0, concat_axis=0, tiled=True)]
    reduce_scatter x0 -> x1, waiting for transfers between devices: none -> 204 us  [body(): return lax.psum_scatter(out, 'expert', scatter_dimension=0, tiled=True)]
    all_gather x1 -> x2, waiting for transfers between devices: 46 us -> 167 us  [the longest x1 167 us: body(): rows = lax.all_gather(tokens, 'expert', axis=0, tiled=True)]
    all_to_all x1, waiting for transfers between devices: 109 us -> 0.01 us  [body(): lax.all_to_all(down_weight[0], 'hidden', split_axis=1, concat_axis=0, til...]
    all_gather x0 -> x1, blocking collectives: none -> 55 us  [body(): weights_all = lax.all_gather(weight_table, 'expert', axis=0, tiled=True)]
    all_to_all x1, starting transfers between devices: 24.9 us -> 4.25 us  [body(): lax.all_to_all(down_weight[0], 'hidden', split_axis=1, concat_axis=0, til...]
    reduce_sum x4 -> x1, other arithmetic: 5.62 us -> 0.11 us  [body(): weight_table = jnp.sum(jnp.where(named, routed[:, :, None], 0.0), axis=1)]
  transfers between devices with their start and end apart: 2 -> 4, of which waited for: 2 -> 2; matrix products, arithmetic and copies ran while one was open for 0% -> 1% of each run, Pallas kernels for 0% -> 0%
where the time goes in v1:
time: 459 us; the launch traced here: 458 us
  waiting for transfers between devices  372 us (81%)
  blocking collectives  55 us (12%)
  between operations  13.2 us (3%)
  matrix products  10.3 us (2%)
    reduce_scatter x1, waiting for transfers between devices, body(): return lax.psum_scatter(out, 'expert', scatter_dimension=0, tiled=True)  204 us
    all_gather x1, waiting for transfers between devices, body(): rows = lax.all_gather(tokens, 'expert', axis=0, tiled=True)  167 us
    all_gather x1, blocking collectives, body(): weights_all = lax.all_gather(weight_table, 'expert', axis=0, tiled=True)  55 us
  transfers between devices with their start and end apart: 4, of which 2 were waited for; matrix products, arithmetic and copies ran while one was open for 1% of the time, Pallas kernels for 0%

profile of v1, /device:TPU:40, one launch (start us, length us, event | category | flops | bytes accessed | tf_op | source)
XLA Modules:
  0.0 458.4 jit_solution(4400639572138969000)
XLA Ops:
  6.5 0.0 all-gather.3.cloned.1.call-start
  6.6 0.7 all-gather.3.cloned.1.call-update
  7.3 0.1 all-gather.5.cloned.1.call-start
  7.4 167.4 %all-gather.3.cloned.1.call-done = bf16[1024,4096]{1,0:T(8,128)(2,1)} async-done(((bf16[16,4096]{1,0:T(8,128)(2,1)}), bf16[1024,4096]{1,0:T(8,128)(2,1)}) %all-gather.3.cloned.1.call-update) | async-done | bytes 8388624 | tf_op jit(solution)/shard_map/all_gather | solution.py:11
  174.8 0.0 copy-start
  174.8 6.5 %fusion.4 = f32[1024,256]{0,1:T(8,128)S(1)} fusion(bf16[1024,4096]{1,0:T(8,128)(2,1)} %all-gather.3.cloned.1.call-done, bf16[4096,128]{1,0:T(8,128)(2,1)} %bitcast.12, bf16[4096,128]{1,0:T(8,128)(2,1)} %bitcast.13), kind=kOutput, calls=%fused_computation.5 | convolution fusion | flops 2151677952 | bytes 11534336 | tf_op jit(solution)/shard_map/dot_general | solution.py:21
  181.3 0.0 copy-start.1
  181.3 0.0 copy-start.2
  181.3 0.9 fusion.7
  182.1 0.1 all-gather.5.cloned.1.call-update
  182.2 0.0 copy-done
  182.2 1.3 copy.19
  183.5 4.2 all-to-all-start
  187.8 0.0 reduce-scatter.2.cloned.1.call-start
  187.8 0.0 copy-done.1
  187.8 0.1 copy.22
  187.9 0.0 copy-done.2
  187.9 0.1 copy.21
  188.0 0.1 select_reduce_fusion
  188.1 55.0 %all_gather.11 = f32[1024,32]{1,0:T(8,128)S(1)} all-gather(f32[16,32]{1,0:T(8,128)S(1)} %select_reduce_fusion), channel_id=1, replica_groups=mesh['groups'=2,'expert'=64,'hidden'=4] {'expert'}, dimensions={0}, use_global_device_ids=true | all-gather | bytes 133120 | tf_op jit(solution)/shard_map/all_gather | solution.py:15
  243.1 0.4 dynamic-slice_reduce_fusion
  243.4 0.0 all-to-all-done
  243.4 0.5 copy.20
  244.0 0.0 all-gather.5.cloned.1.call-done
  244.0 3.9 multiply_convert_fusion
  247.9 0.1 reduce-scatter.2.cloned.1.call-update
  247.9 203.9 %reduce-scatter.2.cloned.1.call-done = bf16[16,1024]{1,0:T(8,128)(2,1)} async-done(((bf16[1024,1024]{1,0:T(8,128)(2,1)}), bf16[16,1024]{1,0:T(8,128)(2,1)}) %reduce-scatter.2.cloned.1.call-update) | async-done | bytes 32784 | tf_op jit(solution)/shard_map/reduce_scatter | solution.py:26
  (2 shorter events, 0.0 us)
Async XLA Ops:
  6.5 168.2 %all-gather.3.cloned.1.call-start = ((), (), s32[]{:S(2)}) async-start(), calls=%async_computation.2 | async-start | bytes 8519680 | tf_op jit(solution)/shard_map/all_gather | solution.py:11
  7.3 236.7 %all-gather.5.cloned.1.call-start = ((), (), s32[]{:S(2)}) async-start(), calls=%async_computation.3 | async-start | bytes 1310720 | tf_op jit(solution)/shard_map/all_gather | solution.py:23
  174.8 7.4 %copy-start = (bf16[1,128,4096]{2,1,0:T(8,128)(2,1)S(1)}, bf16[1,128,4096]{2,1,0:T(8,128)(2,1)}, u32[]{:S(2)}) copy-start(bf16[1,128,4096]{2,1,0:T(8,128)(2,1)} %param.11) | copy-start | bytes 3145732
  181.3 6.5 %copy-start.1 = (f32[16,8]{0,1:T(8,128)S(1)}, f32[16,8]{0,1:T(8,128)}, u32[]{:S(2)}) copy-start(f32[16,8]{0,1:T(8,128)} %param.8) | copy-start | bytes 1540
  181.3 6.6 %copy-start.2 = (s32[16,8]{0,1:T(8,128)S(1)}, s32[16,8]{0,1:T(8,128)}, u32[]{:S(2)}) copy-start(s32[16,8]{0,1:T(8,128)} %param.7) | copy-start | bytes 1540
  183.5 59.9 %all-to-all-start = ((bf16[128,4,1024]{0,2,1:T(8,128)(2,1)}), bf16[128,4,1024]{0,2,1:T(8,128)(2,1)S(1)}, u32[]{:S(2)}, u32[]{:S(2)}) async-start(bf16[128,4,1024]{0,2,1:T(8,128)(2,1)} %bitcast.3), calls=%async_computation | async-start | bytes 2097152 | tf_op jit(solution)/shard_map/all_to_all | solution.py:18
  187.8 264.1 %reduce-scatter.2.cloned.1.call-start = ((), (), s32[]{:S(2)}) async-start(), calls=%async_computation.4 | async-start | bytes 2129920 | tf_op jit(solution)/shard_map/reduce_scatter | solution.py:26
Sparse Core Ops, SparseCore 0:
  9.5 165.2 all-gather.2
  182.3 31.5 all-gather.4
  248.1 203.7 reduce-scatter.1

commit v2 on v1

v2 whole, which is shorter than its diff:
```python
import jax
import jax.numpy as jnp
from jax import lax
from jax.experimental import pallas as pl
from jax.experimental.pallas import tpu as pltpu
from jax.sharding import PartitionSpec as P


SPAN = 2
CAP = 8
F32 = jnp.float32
BF = jnp.bfloat16
VM = pltpu.MemorySpace.VMEM


def pack_kernel(x_ref, ids_ref, scores_ref, tok_ref, out_ref, weight_ref):
    top, count = ids_ref.shape
    experts, halves, cap, part = out_ref.shape
    pairs = experts * cap
    scores = scores_ref[...]
    routed = 2.5 * scores / jnp.sum(scores, axis=0, keepdims=True)
    row = lax.broadcasted_iota(jnp.int32, (pairs, count), 0)
    expert = row // cap
    member = jnp.zeros((pairs, count), F32)
    weight = jnp.zeros((pairs, count), F32)
    for k in range(top):
        hit = ids_ref[k : k + 1, :] == expert
        member = jnp.where(hit, 1.0, member)
        weight = jnp.where(hit, routed[k : k + 1, :], weight)
    earlier = lax.broadcasted_iota(jnp.int32, (count, count), 0) < lax.broadcasted_iota(
        jnp.int32, (count, count), 1
    )
    place = jnp.dot(
        member.astype(BF), jnp.where(earlier, 1.0, 0.0).astype(BF), preferred_element_type=F32
    )
    mine = (member > 0.5) & (place == (row - expert * cap).astype(F32))
    weight_ref[...] = jnp.where(mine, weight, 0.0)
    chosen = jnp.where(mine, 1.0, 0.0).astype(BF)
    for h in range(halves):
        col = pl.multiple_of(x_ref[0] * (halves * part) + h * part, part)
        rows = jnp.dot(chosen, tok_ref[:, pl.ds(col, part)], preferred_element_type=F32)
        for e in range(experts):
            out_ref[e, h] = rows[e * cap : (e + 1) * cap].astype(BF)


def pack(x, ids, scores, tokens, experts, part):
    count = tokens.shape[0]
    return pl.pallas_call(
        pack_kernel,
        out_shape=(
            jax.ShapeDtypeStruct((experts, SPAN, CAP, part), BF),
            jax.ShapeDtypeStruct((experts * CAP, count), F32),
        ),
        in_specs=[pl.BlockSpec(memory_space=pltpu.MemorySpace.SMEM)] + [pl.BlockSpec(memory_space=VM)] * 3,
        out_specs=[pl.BlockSpec(memory_space=VM)] * 2,
        compiler_params=pltpu.CompilerParams(vmem_limit_bytes=24 << 20),
        name="pack",
    )(x, ids, scores, tokens)


def act_kernel(at_ref, *refs):
    piece_refs, gate_ref, up_ref, out_ref = refs[:10], refs[10], refs[11], refs[12]
    part = piece_refs[0].shape[1]
    full = piece_refs[0].shape[0]
    half = full // 2

    def weights(i):
        rows = pl.ds(pl.multiple_of(at_ref[i] * part, part), part)
        return gate_ref[rows, :], up_ref[rows, :]

    def product(i, rows):
        gate, up = weights(i)
        return (
            jnp.dot(rows, gate, preferred_element_type=F32),
            jnp.dot(rows, up, preferred_element_type=F32),
        )

    for b in range(2):
        gate_val = up_val = None
        for core in range(2):
            own, left, right, far_top, far_low = piece_refs[core * 5 : core * 5 + 5]
            far = (far_top, far_low)[b]
            for d, rows in enumerate((own[b * half : (b + 1) * half], left[b * half : (b + 1) * half],
                                      right[b * half : (b + 1) * half], far[...])):
                g, u = product(core * 4 + d, rows)
                gate_val = g if gate_val is None else gate_val + g
                up_val = u if up_val is None else up_val + u
        out_ref[b * half : (b + 1) * half, :] = (gate_val / (1.0 + jnp.exp(-gate_val)) * up_val).astype(BF)


def act_of(at, pieces, gate, up):
    return pl.pallas_call(
        act_kernel,
        out_shape=jax.ShapeDtypeStruct((pieces[0].shape[0], gate.shape[1]), BF),
        in_specs=[pl.BlockSpec(memory_space=pltpu.MemorySpace.SMEM)] + [pl.BlockSpec(memory_space=VM)] * 12,
        out_specs=pl.BlockSpec(memory_space=VM),
        compiler_params=pltpu.CompilerParams(vmem_limit_bytes=24 << 20),
        name="act",
    )(at, *pieces, gate, up)


def down_kernel(at_ref, own_ref, other_ref, keep_ref, got_ref, out_ref):
    blocks, width, part = keep_ref.shape
    own = jnp.concatenate([own_ref[at_ref[i]] for i in range(blocks)], axis=1)
    other = jnp.concatenate([other_ref[at_ref[i]] for i in range(blocks)], axis=1)
    keep = keep_ref[...].reshape(blocks * width, part)
    got = got_ref[...].reshape(blocks * width, part)
    val = jnp.dot(own, keep, preferred_element_type=F32)
    val = val + jnp.dot(other, got, preferred_element_type=F32)
    out_ref[...] = val.astype(BF)


def down_of(at, own, other, keep, got):
    return pl.pallas_call(
        down_kernel,
        out_shape=jax.ShapeDtypeStruct((own.shape[1], keep.shape[2]), BF),
        in_specs=[pl.BlockSpec(memory_space=pltpu.MemorySpace.SMEM)] + [pl.BlockSpec(memory_space=VM)] * 4,
        out_specs=pl.BlockSpec(memory_space=VM),
        compiler_params=pltpu.CompilerParams(vmem_limit_bytes=24 << 20),
        name="down",
    )(at, own, other, keep, got)


def combine_kernel(back_ref, weight_ref, out_ref):
    experts, halves, _, part = back_ref.shape
    weight = weight_ref[...]
    high = weight.astype(BF)
    rest = weight - high.astype(F32)
    middle = rest.astype(BF)
    low = (rest - middle.astype(F32)).astype(BF)
    over_rows = (((0,), (0,)), ((), ()))
    for h in range(halves):
        rows = jnp.concatenate([back_ref[e, h].astype(F32) for e in range(experts)], axis=0).astype(BF)
        val = None
        for term in (low, middle, high):
            more = lax.dot_general(term, rows, over_rows, preferred_element_type=F32)
            val = more if val is None else val + more
        out_ref[:, h * part : (h + 1) * part] = val.astype(BF)


def combine(back, weight):
    return pl.pallas_call(
        combine_kernel,
        out_shape=jax.ShapeDtypeStruct((weight.shape[1], back.shape[1] * back.shape[3]), BF),
        in_specs=[pl.BlockSpec(memory_space=VM)] * 2,
        out_specs=pl.BlockSpec(memory_space=VM),
        compiler_params=pltpu.CompilerParams(vmem_limit_bytes=24 << 20),
        name="combine",
    )(back, weight)


def body(tokens, expert_ids, router_scores, gate_weight, up_weight, down_weight):
    model_width = tokens.shape[1]
    slots, columns = lax.axis_size("expert"), lax.axis_size("hidden")
    experts = slots // SPAN
    part = model_width // (columns * SPAN)
    x = lax.axis_index("hidden").astype(jnp.int32)
    core = (lax.axis_index("expert") % SPAN).astype(jnp.int32)
    swap = [(i, i ^ 1) for i in range(slots)]
    up_x = [(i, (i + 1) % columns) for i in range(columns)]
    down_x = [(i, (i - 1) % columns) for i in range(columns)]

    def swapped(v):
        return lax.ppermute(v, "expert", swap)

    down = down_weight[0]
    arrived = [lax.dynamic_slice_in_dim(down, x * SPAN * part, SPAN * part, 1)]
    for s in range(1, columns):
        share = lax.dynamic_slice_in_dim(down, (x + s) % columns * SPAN * part, SPAN * part, 1)
        arrived.append(lax.ppermute(share, "hidden", [(i, (i + s) % columns) for i in range(columns)]))
    outgoing, weight = pack(
        x.reshape(1), expert_ids.T, router_scores.T, tokens, experts, part
    )
    own = lax.all_to_all(
        outgoing.reshape(slots, CAP, part), "expert", split_axis=0, concat_axis=0, tiled=True
    ).reshape(slots * CAP, part)
    half = slots * CAP // 2
    left = lax.ppermute(own, "hidden", up_x)
    right = lax.ppermute(own, "hidden", down_x)
    far_top = lax.ppermute(left[:half], "hidden", up_x)
    far_low = lax.ppermute(right[half:], "hidden", down_x)
    mine = (own, left, right, far_top, far_low)
    pieces = mine + tuple(swapped(v) for v in mine)
    turns = jnp.array([0, columns - 1, 1, 2], jnp.int32)
    at = ((x + turns) % columns) * SPAN
    at = jnp.concatenate([at + core, at + 1 - core])
    spread = jnp.stack(arrived)
    down_keep = lax.dynamic_slice_in_dim(spread, core * part, part, 2)
    down_got = swapped(lax.dynamic_slice_in_dim(spread, (1 - core) * part, part, 2))
    source = (x - jnp.arange(columns, dtype=jnp.int32)) % columns
    act = act_of(at, pieces, gate_weight[0], up_weight[0])
    act_own = lax.all_gather(act, "hidden", axis=0, tiled=False)
    act_other = swapped(act_own)
    val = down_of(source, act_own, act_other, down_keep, down_got)
    back = lax.all_to_all(
        val.reshape(slots, CAP, part), "expert", split_axis=0, concat_axis=0, tiled=True
    )
    return combine(back.reshape(experts, SPAN, CAP, part), weight)


def solution(mesh):
    return jax.shard_map(
        body,
        mesh=mesh,
        in_specs=(
            P(("groups", "expert"), None),
            P(("groups", "expert"), None),
            P(("groups", "expert"), None),
            P("expert", None, "hidden"),
            P("expert", None, "hidden"),
            P("expert", "hidden", None),
        ),
        out_specs=P(("groups", "expert"), "hidden"),
        check_vma=False,
    )
```

time: 459 us -> 252 us (0.55)
  waiting for transfers between devices: 372 us -> 7.03 us
  blocking collectives: 55 us -> 195 us
  starting transfers between devices: 4.31 us -> 40.4 us
  between operations: 13.2 us -> 0.37 us
  matrix products: 10.3 us -> 0 us
  Pallas kernels: 0 us -> 5.57 us
    reduce_scatter x1 -> x0, waiting for transfers between devices: 204 us -> none  [body(): return lax.psum_scatter(out, 'expert', scatter_dimension=0, tiled=True)]
    all_to_all x0 -> x2, blocking collectives: none -> 181 us  [the longest x1 111 us: body(): lax.all_to_all(outgoing.reshape(slots, CAP, part), 'expert', split_axis=0...]
    all_gather x2 -> x0, waiting for transfers between devices: 167 us -> none  [the longest x1 167 us: body(): rows = lax.all_gather(tokens, 'expert', axis=0, tiled=True)]
    all_gather x1, blocking collectives: 55 us -> 13.7 us  [body(): act_own = lax.all_gather(act, 'hidden', axis=0, tiled=False)]
    ppermute x0 -> x14, starting transfers between devices: none -> 40.4 us  [the longest x7 14.7 us: swapped(): return lax.ppermute(v, 'expert', swap)]
    dot_general x2 -> x0, matrix products: 10.3 us -> none  [the longest x1 6.48 us: body(): val = jnp.dot(rows, both, preferred_element_type=jnp.float32)]
    ppermute x0 -> x14, waiting for transfers between devices: none -> 7.03 us  [the longest x3 4.86 us: body(): lax.ppermute(share, 'hidden', [(i, (i + s) % columns) for i in range(colu...]
    pallas_call x0 -> x4, Pallas kernels: none -> 5.57 us  [the longest x1 2.94 us: act_of(): pl.pallas_call(act_kernel, out_shape=jax.ShapeDtypeStruct((pieces[0].shap...]
  transfers between devices with their start and end apart: 4 -> 14, of which waited for: 2 -> 3; matrix products, arithmetic and copies ran while one was open for 1% -> 0% of each run, Pallas kernels for 0% -> 1%
where the time goes in v2:
time: 252 us
  blocking collectives  195 us (77%)
  starting transfers between devices  40.4 us (16%)
  waiting for transfers between devices  7.03 us (3%)
  Pallas kernels  5.57 us (2%)
  local copies, waits for them, and re-layouts  3.23 us (1%)
    all_to_all x1, blocking collectives, body(): lax.all_to_all(outgoing.reshape(slots, CAP, part), 'expert', split_axis=0...  111 us
    all_to_all x1, blocking collectives, body(): lax.all_to_all(val.reshape(slots, CAP, part), 'expert', split_axis=0, con...  69.9 us
    ppermute x7, starting transfers between devices, swapped(): return lax.ppermute(v, 'expert', swap)  14.7 us
    all_gather x1, blocking collectives, body(): act_own = lax.all_gather(act, 'hidden', axis=0, tiled=False)  13.7 us
    ppermute x3, starting transfers between devices, body(): lax.ppermute(share, 'hidden', [(i, (i + s) % columns) for i in range(colu...  9.3 us
    ppermute x1, starting transfers between devices, body(): far_low = lax.ppermute(right[half:], 'hidden', down_x)  5.66 us
  transfers between devices with their start and end apart: 14, of which 3 were waited for; matrix products, arithmetic and copies ran while one was open for 0% of the time, Pallas kernels for 1%

profile of v2, /device:TPU:40, one launch (start us, length us, event | category | flops | bytes accessed | tf_op | source)
XLA Modules:
  0.0 251.8 jit_solution(8455770498595518827)
XLA Ops:
  0.0 0.7 copy-done.4
  0.7 0.0 copy-done.3
  0.7 0.9 copy-done.2
  1.6 0.4 pack.1
  2.0 111.4 %all_to_all.10 = bf16[64,8,512]{2,1,0:T(8,128)(2,1)S(1)} all-to-all(bf16[64,8,512]{2,1,0:T(8,128)(2,1)S(1)} %bitcast.29), channel_id=1, replica_groups=mesh['groups'=2,'expert'=64,'hidden'=4] {'expert'}, dimensions={0} | all-to-all | bytes 1048576 | tf_op jit(solution)/shard_map/all_to_all | solution.py:174
  113.4 3.6 %collective-permute-start = (bf16[512,512]{1,0:T(8,128)(2,1)S(1)}, bf16[512,512]{1,0:T(8,128)(2,1)S(1)}, u32[]{:S(2)}, u32[]{:S(2)}) collective-permute-start(bf16[512,512]{1,0:T(8,128)(2,1)S(1)} %bitcast.19), channel_id=1, source_target_pairs={{0,1},{1,2},{2,3},{3,0},{4,5},{5,6},{6,7},{7,4},{8,9},{9,10},{10,1... | collective-permute-start | bytes 1572872 | tf_op jit(solution)/shard_map/ppermute | solution.py:178
  117.0 3.5 %collective-permute-start.1 = (bf16[512,512]{1,0:T(8,128)(2,1)S(1)}, bf16[512,512]{1,0:T(8,128)(2,1)S(1)}, u32[]{:S(2)}, u32[]{:S(2)}) collective-permute-start(bf16[512,512]{1,0:T(8,128)(2,1)S(1)} %bitcast.20), channel_id=1, source_target_pairs={{0,3},{1,0},{2,1},{3,2},{4,7},{5,4},{6,5},{7,6},{8,11},{9,8},{10,9... | collective-permute-start | bytes 1572872 | tf_op jit(solution)/shard_map/ppermute | solution.py:179
  120.6 0.0 copy-done.5
  120.6 0.8 constant_dynamic-slice_fusion.2
  121.4 3.9 %collective-permute-start.12 = (bf16[128,1024]{1,0:T(8,128)(2,1)}, bf16[128,1024]{1,0:T(8,128)(2,1)S(1)}, u32[]{:S(2)}, u32[]{:S(2)}) collective-permute-start(bf16[128,1024]{1,0:T(8,128)(2,1)} %get-tuple-element.15), channel_id=1, source_target_pairs={{0,3},{1,0},{2,1},{3,2},{4,7},{5,4},{6,5},{7,6},{8,11},{9,8},{10,9... | collective-permute-start | bytes 786440 | tf_op jit(solution)/shard_map/ppermute | solution.py:170
  125.3 2.5 collective-permute-start.11
  127.8 2.9 %collective-permute-start.10 = (bf16[128,1024]{1,0:T(8,128)(2,1)S(1)}, bf16[128,1024]{1,0:T(8,128)(2,1)S(1)}, u32[]{:S(2)}, u32[]{:S(2)}) collective-permute-start(bf16[128,1024]{1,0:T(8,128)(2,1)S(1)} %get-tuple-element.14), channel_id=1, source_target_pairs={{0,1},{1,2},{2,3},{3,0},{4,5},{5,6},{6,7},{7,4},{8,9},{9,10},{10,1... | collective-permute-start | bytes 786440 | tf_op jit(solution)/shard_map/ppermute | solution.py:170
  130.7 0.0 copy-start.6
  130.8 0.6 copy-done.6
  131.4 0.0 collective-permute-done.refs_1_
  131.4 1.9 collective-permute-start.4
  133.4 0.3 collective-permute-done.1.refs_2_
  133.7 3.6 %collective-permute-start.2 = (bf16[256,512]{1,0:T(8,128)(2,1)S(1)}, bf16[256,512]{1,0:T(8,128)(2,1)S(1)}, u32[]{:S(2)}, u32[]{:S(2)}) collective-permute-start(bf16[256,512]{1,0:T(8,128)(2,1)S(1)} %slice.8), channel_id=1, source_target_pairs={{0,1},{1,2},{2,3},{3,0},{4,5},{5,6},{6,7},{7,4},{8,9},{9,10},{10,1... | collective-permute-start | bytes 786440 | tf_op jit(solution)/shard_map/ppermute | solution.py:180
  137.3 4.9 %collective-permute-done.12 = bf16[128,1024]{1,0:T(8,128)(2,1)S(1)} collective-permute-done((bf16[128,1024]{1,0:T(8,128)(2,1)}, bf16[128,1024]{1,0:T(8,128)(2,1)S(1)}, u32[]{:S(2)}, u32[]{:S(2)}) %collective-permute-start.12) | collective-permute-done | bytes 262176 | tf_op jit(solution)/shard_map/ppermute | solution.py:170
  142.2 5.7 %collective-permute-start.3 = (bf16[256,512]{1,0:T(8,128)(2,1)S(1)}, bf16[256,512]{1,0:T(8,128)(2,1)S(1)}, u32[]{:S(2)}, u32[]{:S(2)}) collective-permute-start(bf16[256,512]{1,0:T(8,128)(2,1)S(1)} %slice.9), channel_id=1, source_target_pairs={{0,3},{1,0},{2,1},{3,2},{4,7},{5,4},{6,5},{7,6},{8,11},{9,8},{10,9... | collective-permute-start | bytes 786440 | tf_op jit(solution)/shard_map/ppermute | solution.py:181
  147.8 0.0 collective-permute-done.11
  147.8 2.0 collective-permute-start.5
  149.8 0.0 collective-permute-done.10
  149.8 2.4 collective-permute-start.6
  152.3 0.1 pad_add_fusion.at_ref
  152.4 0.0 collective-permute-done.2.refs_3_
  152.4 1.9 collective-permute-start.7
  154.3 0.0 collective-permute-done.3.refs_4_
  154.3 2.4 collective-permute-start.8
  156.8 0.1 pad_maximum_fusion
  156.9 0.0 copy-start
  156.9 0.0 copy-start.1
  156.9 0.1 constant_dynamic-slice_fusion
  157.0 0.0 collective-permute-done.4.refs_5_
  157.1 2.1 collective-permute-start.13
  159.1 0.0 collective-permute-done.5.refs_6_
  159.2 0.0 collective-permute-done.6.refs_7_
  159.2 0.0 collective-permute-done.7.refs_8_
  159.2 0.0 collective-permute-done.8.refs_9_
  159.2 0.0 copy-done
  159.2 2.9 %act.1 = bf16[512,128]{1,0:T(8,128)(2,1)S(1)} custom-call(s32[8]{0:T(128)S(1)} %pad_add_fusion.at_ref, bf16[512,512]{1,0:T(8,128)(2,1)S(1)} %bitcast.22, bf16[512,512]{1,0:T(8,128)(2,1)S(1)} %collective-permute-done.refs_1_, bf16[512,512]{1,0:T(8,128)(2,1)S(1)} %collective-permute-done.1.refs_2_, bf16[256,512]{1,0:T(8,128)(2,1)S(1)} %collective-permute-done.2.refs_3_, ...), custom_call_target="tpu_custom_call" | custom-call | tf_op jit(solution)/shard_map/act/pallas_call | solution.py:92
  162.2 13.7 %all-gather = bf16[2048,128]{1,0:T(8,128)(2,1)S(1)} all-gather(bf16[512,128]{1,0:T(8,128)(2,1)S(1)} %act.1), channel_id=2, replica_groups=mesh['groups'=2,'expert'=64,'hidden'=4] {'hidden'}, dimensions={0}, use_global_device_ids=true | all-gather | bytes 655360 | tf_op jit(solution)/shard_map/all_gather | solution.py:192
  175.8 1.9 collective-permute-start.9
  177.8 0.0 collective-permute-done.13.got_ref
  177.8 1.9 collective-permute-done.9.other_ref
  179.7 1.2 down.1
  180.9 69.9 %all_to_all.11 = bf16[64,8,512]{2,1,0:T(8,128)(2,1)S(1)} all-to-all(bf16[64,8,512]{2,1,0:T(8,128)(2,1)S(1)} %bitcast.26), channel_id=1, replica_groups=mesh['groups'=2,'expert'=64,'hidden'=4] {'expert'}, dimensions={0} | all-to-all | bytes 1048576 | tf_op jit(solution)/shard_map/all_to_all | solution.py:195
  250.9 1.0 combine.1
  (10 shorter events, 0.1 us)
Async XLA Ops:
  0.0 0.7 copy-start.4
  0.0 0.7 copy-start.3
  0.7 0.9 copy-start.2
  1.6 119.0 %copy-start.5 = (bf16[1,128,4096]{2,1,0:T(8,128)(2,1)S(1)}, bf16[1,128,4096]{2,1,0:T(8,128)(2,1)}, u32[]{:S(2)}) copy-start(bf16[1,128,4096]{2,1,0:T(8,128)(2,1)} %param.12) | copy-start | bytes 3145732
  113.4 18.0 %collective-permute-start = (bf16[512,512]{1,0:T(8,128)(2,1)S(1)}, bf16[512,512]{1,0:T(8,128)(2,1)S(1)}, u32[]{:S(2)}, u32[]{:S(2)}) collective-permute-start(bf16[512,512]{1,0:T(8,128)(2,1)S(1)} %bitcast.19), channel_id=1, source_target_pairs={{0,1},{1,2},{2,3},{3,0},{4,5},{5,6},{6,7},{7,4},{8,9},{9,10},{10,1... | collective-permute-start | bytes 1572872 | tf_op jit(solution)/shard_map/ppermute | solution.py:178
  117.0 16.7 %collective-permute-start.1 = (bf16[512,512]{1,0:T(8,128)(2,1)S(1)}, bf16[512,512]{1,0:T(8,128)(2,1)S(1)}, u32[]{:S(2)}, u32[]{:S(2)}) collective-permute-start(bf16[512,512]{1,0:T(8,128)(2,1)S(1)} %bitcast.20), channel_id=1, source_target_pairs={{0,3},{1,0},{2,1},{3,2},{4,7},{5,4},{6,5},{7,6},{8,11},{9,8},{10,9... | collective-permute-start | bytes 1572872 | tf_op jit(solution)/shard_map/ppermute | solution.py:179
  121.4 20.8 %collective-permute-start.12 = (bf16[128,1024]{1,0:T(8,128)(2,1)}, bf16[128,1024]{1,0:T(8,128)(2,1)S(1)}, u32[]{:S(2)}, u32[]{:S(2)}) collective-permute-start(bf16[128,1024]{1,0:T(8,128)(2,1)} %get-tuple-element.15), channel_id=1, source_target_pairs={{0,3},{1,0},{2,1},{3,2},{4,7},{5,4},{6,5},{7,6},{8,11},{9,8},{10,9... | collective-permute-start | bytes 786440 | tf_op jit(solution)/shard_map/ppermute | solution.py:170
  125.3 22.6 %collective-permute-start.11 = (bf16[128,1024]{1,0:T(8,128)(2,1)S(1)}, bf16[128,1024]{1,0:T(8,128)(2,1)S(1)}, u32[]{:S(2)}, u32[]{:S(2)}) collective-permute-start(bf16[128,1024]{1,0:T(8,128)(2,1)S(1)} %get-tuple-element.16), channel_id=1, source_target_pairs={{0,2},{1,3},{2,0},{3,1},{4,6},{5,7},{6,4},{7,5},{8,10},{9,11},{10,... | collective-permute-start | bytes 786440 | tf_op jit(solution)/shard_map/ppermute | solution.py:170
  127.8 22.0 %collective-permute-start.10 = (bf16[128,1024]{1,0:T(8,128)(2,1)S(1)}, bf16[128,1024]{1,0:T(8,128)(2,1)S(1)}, u32[]{:S(2)}, u32[]{:S(2)}) collective-permute-start(bf16[128,1024]{1,0:T(8,128)(2,1)S(1)} %get-tuple-element.14), channel_id=1, source_target_pairs={{0,1},{1,2},{2,3},{3,0},{4,5},{5,6},{6,7},{7,4},{8,9},{9,10},{10,1... | collective-permute-start | bytes 786440 | tf_op jit(solution)/shard_map/ppermute | solution.py:170
  130.7 0.7 copy-start.6
  131.4 25.6 %collective-permute-start.4 = (bf16[512,512]{1,0:T(8,128)(2,1)S(1)}, bf16[512,512]{1,0:T(8,128)(2,1)S(1)}, u32[]{:S(2)}, u32[]{:S(2)}) collective-permute-start(bf16[512,512]{1,0:T(8,128)(2,1)S(1)} %bitcast.21), channel_id=1, source_target_pairs={{0,4},{4,0},{8,12},{12,8},{16,20},{20,16},{24,28},{28,24},{32,36},... | collective-permute-start | bytes 1572872 | tf_op jit(solution)/shard_map/ppermute | solution.py:164
  133.7 18.7 %collective-permute-start.2 = (bf16[256,512]{1,0:T(8,128)(2,1)S(1)}, bf16[256,512]{1,0:T(8,128)(2,1)S(1)}, u32[]{:S(2)}, u32[]{:S(2)}) collective-permute-start(bf16[256,512]{1,0:T(8,128)(2,1)S(1)} %slice.8), channel_id=1, source_target_pairs={{0,1},{1,2},{2,3},{3,0},{4,5},{5,6},{6,7},{7,4},{8,9},{9,10},{10,1... | collective-permute-start | bytes 786440 | tf_op jit(solution)/shard_map/ppermute | solution.py:180
  142.2 12.1 %collective-permute-start.3 = (bf16[256,512]{1,0:T(8,128)(2,1)S(1)}, bf16[256,512]{1,0:T(8,128)(2,1)S(1)}, u32[]{:S(2)}, u32[]{:S(2)}) collective-permute-start(bf16[256,512]{1,0:T(8,128)(2,1)S(1)} %slice.9), channel_id=1, source_target_pairs={{0,3},{1,0},{2,1},{3,2},{4,7},{5,4},{6,5},{7,6},{8,11},{9,8},{10,9... | collective-permute-start | bytes 786440 | tf_op jit(solution)/shard_map/ppermute | solution.py:181
  147.8 11.3 %collective-permute-start.5 = (bf16[512,512]{1,0:T(8,128)(2,1)S(1)}, bf16[512,512]{1,0:T(8,128)(2,1)S(1)}, u32[]{:S(2)}, u32[]{:S(2)}) collective-permute-start(bf16[512,512]{1,0:T(8,128)(2,1)S(1)} %collective-permute-done.refs_1_), channel_id=1, source_target_pairs={{0,4},{4,0},{8,12},{12,8},{16,20},{20,16},{24,28},{28,24},{32,36},... | collective-permute-start | bytes 1572872 | tf_op jit(solution)/shard_map/ppermute | solution.py:164
  149.8 9.3 %collective-permute-start.6 = (bf16[512,512]{1,0:T(8,128)(2,1)S(1)}, bf16[512,512]{1,0:T(8,128)(2,1)S(1)}, u32[]{:S(2)}, u32[]{:S(2)}) collective-permute-start(bf16[512,512]{1,0:T(8,128)(2,1)S(1)} %collective-permute-done.1.refs_2_), channel_id=1, source_target_pairs={{0,4},{4,0},{8,12},{12,8},{16,20},{20,16},{24,28},{28,24},{32,36},... | collective-permute-start | bytes 1572872 | tf_op jit(solution)/shard_map/ppermute | solution.py:164
  152.4 6.8 %collective-permute-start.7 = (bf16[256,512]{1,0:T(8,128)(2,1)S(1)}, bf16[256,512]{1,0:T(8,128)(2,1)S(1)}, u32[]{:S(2)}, u32[]{:S(2)}) collective-permute-start(bf16[256,512]{1,0:T(8,128)(2,1)S(1)} %collective-permute-done.2.refs_3_), channel_id=1, source_target_pairs={{0,4},{4,0},{8,12},{12,8},{16,20},{20,16},{24,28},{28,24},{32,36},... | collective-permute-start | bytes 786440 | tf_op jit(solution)/shard_map/ppermute | solution.py:164
  154.3 4.9 %collective-permute-start.8 = (bf16[256,512]{1,0:T(8,128)(2,1)S(1)}, bf16[256,512]{1,0:T(8,128)(2,1)S(1)}, u32[]{:S(2)}, u32[]{:S(2)}) collective-permute-start(bf16[256,512]{1,0:T(8,128)(2,1)S(1)} %collective-permute-done.3.refs_4_), channel_id=1, source_target_pairs={{0,4},{4,0},{8,12},{12,8},{16,20},{20,16},{24,28},{28,24},{32,36},... | collective-permute-start | bytes 786440 | tf_op jit(solution)/shard_map/ppermute | solution.py:164
  156.9 2.3 copy-start
  156.9 2.3 copy-start.1
  157.1 20.8 %collective-permute-start.13 = (bf16[4,128,512]{2,1,0:T(8,128)(2,1)S(1)}, bf16[4,128,512]{2,1,0:T(8,128)(2,1)S(1)}, u32[]{:S(2)}, u32[]{:S(2)}) collective-permute-start(bf16[4,128,512]{2,1,0:T(8,128)(2,1)S(1)} %get-tuple-element.11), channel_id=1, source_target_pairs={{0,4},{4,0},{8,12},{12,8},{16,20},{20,16},{24,28},{28,24},{32,36},... | collective-permute-start | bytes 1572872 | tf_op jit(solution)/shard_map/ppermute | solution.py:164
  175.8 3.8 %collective-permute-start.9 = (bf16[4,512,128]{2,1,0:T(8,128)(2,1)S(1)}, bf16[4,512,128]{2,1,0:T(8,128)(2,1)S(1)}, u32[]{:S(2)}, u32[]{:S(2)}) collective-permute-start(bf16[4,512,128]{2,1,0:T(8,128)(2,1)S(1)} %bitcast.23), channel_id=1, source_target_pairs={{0,4},{4,0},{8,12},{12,8},{16,20},{20,16},{24,28},{28,24},{32,36},... | collective-permute-start | bytes 1572872 | tf_op jit(solution)/shard_map/ppermute | solution.py:164
